TPU v7x, 32 devices: a whole 2x2x4 slice. The times are simulated.
32 devices in a mesh: row: 4 (over x, core), col: 8 (over z, y).
Axes of the slice: x: 2, y: 2, z: 4, core: 2. Of those that a mesh axis runs over, the one named last changes fastest.
Arguments:
- tensor: float32 [1024, 32, 1024], P(None, 'row', 'col'), may hold values from -60 to 60, as said below
- factor_two: float32 [32, 32], P('row'), may hold values from -1 to 1
- factor_three: float32 [32, 32], P('col'), may hold values from -1 to 1
- factor_four: float32 [32, 16], replicated, may hold values from -1 to 1
- factor_init: float32 [1024, 64], replicated, may hold values from -6 to 6
Outputs:
- factor_new: float32 [1024, 64], replicated
- core: float32 [64, 32, 32, 16], P(None, 'row', 'col')
Inputs may be any that keep to these rules, and one draw needn't show every extreme that they name: `tensor`: scales vary from slab to slab.
All inputs are finite; a program needn't handle non-finite values.
Results may differ from a plain program's by a relative error of at most 0.00013.
Values sent between devices are 32-bit elements; how exact they have to be, the bound alone decides.
A program may use at most 128 MiB of HBM per device.

v0:
```python
import jax
import jax.numpy as jnp
from jax import lax
from jax.sharding import PartitionSpec as P


def shards(tensor, factor_two, factor_three, factor_four, factor_init):
    highest = lax.Precision.HIGHEST
    first_len = tensor.shape[0]
    local_two = tensor.shape[1]
    fourth_len = factor_four.shape[0]
    local_three = tensor.shape[2] // fourth_len
    rank_one = factor_init.shape[1]
    data = tensor.reshape(first_len, local_two, local_three, fourth_len)
    fourth = jnp.einsum("abcd,de->abce", data, factor_four, precision=highest)
    whole_two = lax.all_gather(factor_two, "row", axis=0, tiled=True)
    spread_two = lax.all_to_all(fourth, "row", split_axis=0, concat_axis=1, tiled=True)
    projected_two = jnp.einsum("abce,bg->agce", spread_two, whole_two, precision=highest)
    partial_two = lax.all_to_all(projected_two, "row", split_axis=1, concat_axis=0, tiled=True)
    whole_three = lax.all_gather(factor_three, "col", axis=0, tiled=True)
    spread_three = lax.all_to_all(partial_two, "col", split_axis=0, concat_axis=2, tiled=True)
    projected_three = jnp.einsum("agce,cf->agfe", spread_three, whole_three, precision=highest)
    block = lax.all_to_all(projected_three, "col", split_axis=2, concat_axis=0, tiled=True)
    columns = block.reshape(first_len, -1)
    basis = factor_init
    local_gram = jnp.dot(columns, columns.T, precision=highest, preferred_element_type=jnp.float32)
    gram = lax.psum(local_gram, ("row", "col"))
    image = jnp.dot(gram, basis, precision=highest, preferred_element_type=jnp.float32)
    square = jnp.dot(image.T, image, precision=highest, preferred_element_type=jnp.float32)
    lower = jnp.linalg.cholesky(square)
    basis = jax.scipy.linalg.solve_triangular(lower, image.T, lower=True).T
    core = jnp.dot(basis.T, columns, precision=highest, preferred_element_type=jnp.float32)
    return (basis, core.reshape(rank_one, block.shape[1], block.shape[2], block.shape[3]))


def solution(mesh):
    in_specs = (P(None, "row", "col"), P("row", None), P("col", None), P(), P())
    out_specs = (P(), P(None, "row", "col", None))
    return jax.shard_map(shards, mesh=mesh, in_specs=in_specs, out_specs=out_specs, check_vma=False)
```

profile of v0, /device:TPU:0, one launch (start us, length us, event | category | flops | bytes accessed | tf_op | source)
XLA Modules:
  0.0 512.5 jit_solution(1816454857235836736)
XLA Ops:
  7.2 5.5 %copy.18 = f32[1024,8,128]{0,2,1:T(8,128)} copy(f32[1024,8,128]{2,1,0:T(8,128)} %param.5) | data formatting | bytes 8388608 | tf_op args[0]
  12.6 4.2 fusion.12
  16.8 12.2 %copy.19 = f32[1024,8,4,16]{3,2,1,0:T(4,128)} copy(f32[1024,8,4,16]{0,3,2,1:T(8,128)S(1)} %fusion.12) | data formatting | bytes 4194304 | tf_op jit(solution)/shard_map/abcd,de->abce/dot_general | solution.py:15
  29.0 15.5 %reshape.31 = f32[4,1,131072]{2,1,0:T(1,128)} reshape(f32[1024,8,4,16]{3,2,1,0:T(4,128)} %copy.19) | data formatting | bytes 4194304
  44.5 4.4 all-to-all-start
  48.9 26.7 %all_gather.6 = f32[32,32]{1,0:T(8,128)S(1)} all-gather(f32[8,32]{1,0:T(8,128)S(1)} %copy-done.5), channel_id=1, replica_groups=mesh['row'=4,'col'=8] {'row'}, dimensions={0}, use_global_device_ids=true | all-gather | bytes 5120 | tf_op jit(solution)/shard_map/all_gather | solution.py:16
  75.5 1.4 copy-done.2
  77.4 7.7 %reduce.6 = f32[4,131072]{1,0:T(4,128)S(1)} reduce(f32[4,1,131072]{2,1,0:T(1,128)} %copy-done.2, f32[]{:T(128)} %broadcast.53), dimensions={1}, to_apply=%all_to_all.50.reduce_sub_computation | reduce | bytes 4194308 | tf_op jit(solution)/shard_map/all_to_all | solution.py:17
  85.1 17.9 %reshape.32 = f32[1024,8,4,16]{3,2,1,0:T(4,128)} reshape(f32[4,131072]{1,0:T(4,128)S(1)} %reduce.6) | data formatting | bytes 4194304
  103.0 12.2 %copy.20 = f32[4,256,8,4,16]{1,2,0,4,3:T(8,128)S(1)} copy(f32[4,256,8,4,16]{4,3,2,1,0:T(4,128)} %bitcast.72) | data formatting | bytes 4194304 | tf_op jit(solution)/shard_map/all_to_all | solution.py:17
  115.3 1.9 fusion.2
  117.2 1.2 copy.21
  118.4 28.1 %all_to_all.69 = f32[256,32,4,16]{0,3,2,1:T(8,128)S(1)} all-to-all(f32[256,32,4,16]{0,3,2,1:T(8,128)S(1)} %copy.21), channel_id=1, replica_groups=mesh['row'=4,'col'=8] {'row'}, dimensions={1} | all-to-all | bytes 4194304 | tf_op jit(solution)/shard_map/all_to_all | solution.py:19
  146.6 12.1 %copy.37 = f32[256,4,8,4,16]{4,3,2,0,1:T(4,128)} copy(f32[256,4,8,4,16]{0,4,3,2,1:T(8,128)S(1)} %bitcast.78) | data formatting | bytes 4194304 | tf_op jit(solution)/shard_map/all_to_all | solution.py:19
  158.6 15.4 %reshape.33 = f32[8,1,65536]{2,1,0:T(1,128)} reshape(f32[1024,8,4,16]{3,2,1,0:T(4,128)} %bitcast.73) | data formatting | bytes 4194304
  174.0 6.8 %all-to-all-start.2 = ((f32[8,1,65536]{2,1,0:T(1,128)}), f32[8,1,65536]{2,1,0:T(1,128)}, u32[]{:S(2)}, u32[]{:S(2)}) async-start(f32[8,1,65536]{2,1,0:T(1,128)} %reshape.33), calls=%async_computation.2 | async-start | bytes 4194304 | tf_op jit(solution)/shard_map/all_to_all | solution.py:21
  180.9 66.5 %all-gather = f32[8,4,32]{2,1,0:T(4,128)S(1)} all-gather(f32[1,4,32]{2,1,0:T(4,128)S(1)} %bitcast.85), channel_id=1, replica_groups=mesh['row'=4,'col'=8] {'col'}, dimensions={0}, use_global_device_ids=true | all-gather | bytes 4608 | tf_op jit(solution)/shard_map/all_gather | solution.py:20
  247.3 7.2 %reduce.7 = f32[8,65536]{1,0:T(8,128)S(1)} reduce(f32[8,1,65536]{2,1,0:T(1,128)} %all-to-all-done.2, f32[]{:T(128)} %broadcast.53), dimensions={1}, to_apply=%all_to_all.58.reduce_sub_computation | reduce | bytes 4194308 | tf_op jit(solution)/shard_map/all_to_all | solution.py:21
  254.6 17.3 %reshape.34 = f32[1024,8,4,16]{3,2,1,0:T(4,128)} reshape(f32[8,65536]{1,0:T(8,128)S(1)} %reduce.7) | data formatting | bytes 4194304
  271.9 9.8 %copy.35 = f32[8,128,8,4,16]{1,0,4,3,2:T(8,128)S(1)} copy(f32[8,128,8,4,16]{4,3,2,1,0:T(4,128)} %bitcast.74) | data formatting | bytes 4194304 | tf_op jit(solution)/shard_map/all_to_all | solution.py:21
  281.7 1.4 copy.25
  283.1 1.9 convolution_bitcast_fusion
  285.0 1.2 copy.27
  286.2 46.2 %all_to_all.70 = f32[128,8,32,16]{0,3,1,2:T(8,128)S(1)} all-to-all(f32[128,8,32,16]{0,3,1,2:T(8,128)S(1)} %copy.27), channel_id=1, replica_groups=mesh['row'=4,'col'=8] {'col'}, dimensions={2} | all-to-all | bytes 4194304 | tf_op jit(solution)/shard_map/all_to_all | solution.py:23
  332.5 1.2 copy.28
  333.7 8.9 %fusion.14 = f32[1024,1024]{1,0:T(8,128)} fusion(f32[64,8,8,128]{3,2,1,0:T(8,128)S(1)} %bitcast.75), kind=kOutput, calls=%fused_computation.20 | convolution fusion | flops 6442450944 | bytes 6291456 | tf_op jit(solution)/shard_map/dot_general | solution.py:26
  342.7 1.9 copy.41
  344.5 138.8 %all-reduce.2.cloned.1.call-done = f32[1024,1024]{1,0:T(8,128)} async-done(((f32[1024,1024]{1,0:T(8,128)}), f32[1024,1024]{1,0:T(8,128)}) %all-reduce.2.cloned.1.call-update) | async-done | bytes 4194320 | tf_op jit(solution)/shard_map/psum | solution.py:27
  483.4 6.3 %fusion.15 = f32[1024,64]{0,1:T(8,128)S(1)} fusion(f32[1024,1024]{1,0:T(8,128)} %all-reduce.2.cloned.1.call-done, f32[1024,64]{0,1:T(8,128)S(1)} %copy-done), kind=kOutput, calls=%fused_computation.21 | convolution fusion | flops 805306368 | bytes 4718592 | tf_op jit(solution)/shard_map/dot_general | solution.py:28
  490.2 5.8 %cholesky.16 = f32[64,64]{1,0:T(8,128)S(1)} custom-call(f32[64,64]{1,0:T(8,128)S(1)} %fusion.10), custom_call_target="Cholesky" | custom-call | tf_op jit(solution)/shard_map/jit(cholesky)/cholesky | solution.py:30
  497.3 4.9 custom-call.7
  502.7 2.5 fusion.5
  (25 shorter events, 2.8 us)
Async XLA Ops:
  7.2 476.2 %copy-start = (f32[1024,64]{0,1:T(8,128)S(1)}, f32[1024,64]{0,1:T(8,128)}, u32[]{:S(2)}) copy-start(f32[1024,64]{0,1:T(8,128)} %param.9) | copy-start | bytes 786436
  7.2 5.5 %copy-start.4 = (f32[32,16]{0,1:T(8,128)S(1)}, f32[32,16]{0,1:T(8,128)}, u32[]{:S(2)}) copy-start(f32[32,16]{0,1:T(8,128)} %param.8) | copy-start | bytes 6148
  44.5 4.4 copy-start.5
  44.5 31.1 %all-to-all-start = ((f32[4,1,131072]{2,1,0:T(1,128)}), f32[4,1,131072]{2,1,0:T(1,128)S(1)}, u32[]{:S(2)}, u32[]{:S(2)}) async-start(f32[4,1,131072]{2,1,0:T(1,128)} %reshape.31), calls=%async_computation | async-start | bytes 4194304 | tf_op jit(solution)/shard_map/all_to_all | solution.py:17
  75.5 1.4 copy-start.2
  174.0 6.8 %copy-start.6 = (f32[4,32]{1,0:T(4,128)S(1)}, f32[4,32]{1,0:T(4,128)}, u32[]{:S(2)}) copy-start(f32[4,32]{1,0:T(4,128)} %param.7) | copy-start | bytes 1540
  174.0 73.3 %all-to-all-start.2 = ((f32[8,1,65536]{2,1,0:T(1,128)}), f32[8,1,65536]{2,1,0:T(1,128)}, u32[]{:S(2)}, u32[]{:S(2)}) async-start(f32[8,1,65536]{2,1,0:T(1,128)} %reshape.33), calls=%async_computation.2 | async-start | bytes 4194304 | tf_op jit(solution)/shard_map/all_to_all | solution.py:21
  180.8 302.5 %all-reduce.2.cloned.1.call-start = ((), (), s32[]{:S(2)}) async-start(), calls=%async_computation.4 | async-start | bytes 8388608 | tf_op jit(solution)/shard_map/psum | solution.py:27
  344.5 158.2 %copy-start.1 = (f32[64,8,8,128]{3,1,2,0:T(8,128)S(1)}, f32[64,8,8,128]{3,1,2,0:T(8,128)}, u32[]{:S(2)}) copy-start(f32[64,8,8,128]{3,1,2,0:T(8,128)} %copy.41) | copy-start | bytes 6291460
  502.7 2.5 copy-start.3
Sparse Core Ops, SparseCore 0:
  342.8 140.5 all-reduce.1
where the time goes:
time: 518 us; the launch traced here: 512 us
  blocking collectives  168 us (32%)
  waiting for transfers between devices  139 us (27%)
  local copies, waits for them, and re-layouts  127 us (25%)
  other arithmetic  27 us (5%)
  matrix products  26.5 us (5%)
  between operations  14.6 us (3%)
  starting transfers between devices  11.2 us (2%)
    psum x1, waiting for transfers between devices, shards(): gram = lax.psum(local_gram, ('row', 'col'))  139 us
    unnamed x20, local copies, waits for them, and re-layouts  74.8 us
    all_gather x1, blocking collectives, shards(): whole_three = lax.all_gather(factor_three, 'col', axis=0, tiled=True)  66.5 us
    all_to_all x1, blocking collectives, shards(): lax.all_to_all(projected_three, 'col', split_axis=2, concat_axis=0, tiled...  46.2 us
    all_to_all x1, blocking collectives, shards(): lax.all_to_all(projected_two, 'row', split_axis=1, concat_axis=0, tiled=T...  28.1 us
    all_gather x1, blocking collectives, shards(): whole_two = lax.all_gather(factor_two, 'row', axis=0, tiled=True)  26.7 us
    all_to_all x2, local copies, waits for them, and re-layouts, shards(): lax.all_to_all(fourth, 'row', split_axis=0, concat_axis=1, tiled=True)  12.7 us
    dot_general x1, local copies, waits for them, and re-layouts, shards(): fourth = jnp.einsum('abcd,de->abce', data, factor_four, precision=highest)  12.2 us
  transfers between devices with their start and end apart: 3, of which 1 were waited for; matrix products, arithmetic and copies ran while one was open for 0% of the time, Pallas kernels for 0%

commit v1 on v0

--- a/solution.py
+++ b/solution.py
@@ -24,7 +24,9 @@
     columns = block.reshape(first_len, -1)
     basis = factor_init
     local_gram = jnp.dot(columns, columns.T, precision=highest, preferred_element_type=jnp.float32)
-    gram = lax.psum(local_gram, ("row", "col"))
+    gram = local_gram
+    for axis in ("row", "col"):
+        gram = lax.psum(gram, axis)
     image = jnp.dot(gram, basis, precision=highest, preferred_element_type=jnp.float32)
     square = jnp.dot(image.T, image, precision=highest, preferred_element_type=jnp.float32)
     lower = jnp.linalg.cholesky(square)

time: 518 us -> 621 us (1.20)
  waiting for transfers between devices: 139 us -> 242 us
    psum x1 -> x2, waiting for transfers between devices: 139 us -> 242 us  [shards(): gram = lax.psum(gram, axis)]
  transfers between devices with their start and end apart: 3 -> 4, of which waited for: 1 -> 2; matrix products, arithmetic and copies ran while one was open for 0% -> 0% of each run, Pallas kernels for 0% -> 0%
where the time goes in v1:
time: 621 us; the launch traced here: 616 us
  waiting for transfers between devices  242 us (39%)
  blocking collectives  168 us (27%)
  local copies, waits for them, and re-layouts  127 us (20%)
  other arithmetic  27 us (4%)
  matrix products  26.3 us (4%)
  between operations  14.6 us (2%)
  starting transfers between devices  11.5 us (2%)
    psum x2, waiting for transfers between devices, shards(): gram = lax.psum(gram, axis)  242 us
    unnamed x20, local copies, waits for them, and re-layouts  74.8 us
    all_gather x1, blocking collectives, shards(): whole_three = lax.all_gather(factor_three, 'col', axis=0, tiled=True)  66.5 us
    all_to_all x1, blocking collectives, shards(): lax.all_to_all(projected_three, 'col', split_axis=2, concat_axis=0, tiled...  46.2 us
    all_to_all x1, blocking collectives, shards(): lax.all_to_all(projected_two, 'row', split_axis=1, concat_axis=0, tiled=T...  28.1 us
    all_gather x1, blocking collectives, shards(): whole_two = lax.all_gather(factor_two, 'row', axis=0, tiled=True)  26.7 us
    all_to_all x2, local copies, waits for them, and re-layouts, shards(): lax.all_to_all(fourth, 'row', split_axis=0, concat_axis=1, tiled=True)  12.7 us
  transfers between devices with their start and end apart: 4, of which 2 were waited for; matrix products, arithmetic and copies ran while one was open for 0% of the time, Pallas kernels for 0%

profile of v1, /device:TPU:0, one launch (start us, length us, event | category | flops | bytes accessed | tf_op | source)
XLA Modules:
  0.0 615.7 jit_solution(13689654708125370836)
XLA Ops:
  7.2 5.5 copy.18
  12.6 4.2 fusion.12
  16.8 12.2 %copy.19 = f32[1024,8,4,16]{3,2,1,0:T(4,128)} copy(f32[1024,8,4,16]{0,3,2,1:T(8,128)S(1)} %fusion.12) | data formatting | bytes 4194304 | tf_op jit(solution)/shard_map/abcd,de->abce/dot_general | solution.py:15
  29.0 15.5 %reshape.31 = f32[4,1,131072]{2,1,0:T(1,128)} reshape(f32[1024,8,4,16]{3,2,1,0:T(4,128)} %copy.19) | data formatting | bytes 4194304
  44.5 4.4 all-to-all-start
  48.9 26.7 %all_gather.6 = f32[32,32]{1,0:T(8,128)S(1)} all-gather(f32[8,32]{1,0:T(8,128)S(1)} %copy-done.5), channel_id=1, replica_groups=mesh['row'=4,'col'=8] {'row'}, dimensions={0}, use_global_device_ids=true | all-gather | bytes 5120 | tf_op jit(solution)/shard_map/all_gather | solution.py:16
  75.5 1.4 copy-done.2
  77.4 7.7 %reduce.6 = f32[4,131072]{1,0:T(4,128)S(1)} reduce(f32[4,1,131072]{2,1,0:T(1,128)} %copy-done.2, f32[]{:T(128)} %broadcast.53), dimensions={1}, to_apply=%all_to_all.50.reduce_sub_computation | reduce | bytes 4194308 | tf_op jit(solution)/shard_map/all_to_all | solution.py:17
  85.1 17.9 %reshape.32 = f32[1024,8,4,16]{3,2,1,0:T(4,128)} reshape(f32[4,131072]{1,0:T(4,128)S(1)} %reduce.6) | data formatting | bytes 4194304
  103.0 12.2 %copy.20 = f32[4,256,8,4,16]{1,2,0,4,3:T(8,128)S(1)} copy(f32[4,256,8,4,16]{4,3,2,1,0:T(4,128)} %bitcast.72) | data formatting | bytes 4194304 | tf_op jit(solution)/shard_map/all_to_all | solution.py:17
  115.3 1.9 fusion.2
  117.2 1.2 copy.21
  118.4 28.1 %all_to_all.69 = f32[256,32,4,16]{0,3,2,1:T(8,128)S(1)} all-to-all(f32[256,32,4,16]{0,3,2,1:T(8,128)S(1)} %copy.21), channel_id=1, replica_groups=mesh['row'=4,'col'=8] {'row'}, dimensions={1} | all-to-all | bytes 4194304 | tf_op jit(solution)/shard_map/all_to_all | solution.py:19
  146.6 12.1 %copy.37 = f32[256,4,8,4,16]{4,3,2,0,1:T(4,128)} copy(f32[256,4,8,4,16]{0,4,3,2,1:T(8,128)S(1)} %bitcast.78) | data formatting | bytes 4194304 | tf_op jit(solution)/shard_map/all_to_all | solution.py:19
  158.6 15.4 %reshape.33 = f32[8,1,65536]{2,1,0:T(1,128)} reshape(f32[1024,8,4,16]{3,2,1,0:T(4,128)} %bitcast.73) | data formatting | bytes 4194304
  174.0 6.8 %all-to-all-start.2 = ((f32[8,1,65536]{2,1,0:T(1,128)}), f32[8,1,65536]{2,1,0:T(1,128)}, u32[]{:S(2)}, u32[]{:S(2)}) async-start(f32[8,1,65536]{2,1,0:T(1,128)} %reshape.33), calls=%async_computation.2 | async-start | bytes 4194304 | tf_op jit(solution)/shard_map/all_to_all | solution.py:21
  180.9 66.5 %all-gather = f32[8,4,32]{2,1,0:T(4,128)S(1)} all-gather(f32[1,4,32]{2,1,0:T(4,128)S(1)} %bitcast.85), channel_id=1, replica_groups=mesh['row'=4,'col'=8] {'col'}, dimensions={0}, use_global_device_ids=true | all-gather | bytes 4608 | tf_op jit(solution)/shard_map/all_gather | solution.py:20
  247.3 7.2 %reduce.7 = f32[8,65536]{1,0:T(8,128)S(1)} reduce(f32[8,1,65536]{2,1,0:T(1,128)} %all-to-all-done.2, f32[]{:T(128)} %broadcast.53), dimensions={1}, to_apply=%all_to_all.58.reduce_sub_computation | reduce | bytes 4194308 | tf_op jit(solution)/shard_map/all_to_all | solution.py:21
  254.6 17.3 %reshape.34 = f32[1024,8,4,16]{3,2,1,0:T(4,128)} reshape(f32[8,65536]{1,0:T(8,128)S(1)} %reduce.7) | data formatting | bytes 4194304
  271.9 9.8 %copy.35 = f32[8,128,8,4,16]{1,0,4,3,2:T(8,128)S(1)} copy(f32[8,128,8,4,16]{4,3,2,1,0:T(4,128)} %bitcast.74) | data formatting | bytes 4194304 | tf_op jit(solution)/shard_map/all_to_all | solution.py:21
  281.7 1.4 copy.25
  283.1 1.9 convolution_bitcast_fusion
  285.0 1.2 copy.27
  286.2 46.2 %all_to_all.70 = f32[128,8,32,16]{0,3,1,2:T(8,128)S(1)} all-to-all(f32[128,8,32,16]{0,3,1,2:T(8,128)S(1)} %copy.27), channel_id=1, replica_groups=mesh['row'=4,'col'=8] {'col'}, dimensions={2} | all-to-all | bytes 4194304 | tf_op jit(solution)/shard_map/all_to_all | solution.py:23
  333.7 8.7 %fusion.14 = f32[1024,1024]{1,0:T(8,128)} fusion(f32[64,8,8,128]{3,2,1,0:T(8,128)S(1)} %bitcast.75), kind=kOutput, calls=%fused_computation.20 | convolution fusion | flops 6442450944 | bytes 6291456 | tf_op jit(solution)/shard_map/dot_general | solution.py:26
  342.7 83.6 %all-reduce.3.cloned.1.call-done = f32[1024,1024]{1,0:T(8,128)} async-done(((f32[1024,1024]{1,0:T(8,128)}), f32[1024,1024]{1,0:T(8,128)}) %all-reduce.3.cloned.1.call-update) | async-done | bytes 4194320 | tf_op jit(solution)/shard_map/psum | solution.py:29
  426.4 1.9 copy.41
  428.2 158.4 %all-reduce.5.cloned.1.call-done = f32[1024,1024]{1,0:T(8,128)} async-done(((f32[1024,1024]{1,0:T(8,128)}), f32[1024,1024]{1,0:T(8,128)}) %all-reduce.5.cloned.1.call-update) | async-done | bytes 4194320 | tf_op jit(solution)/shard_map/psum | solution.py:29
  586.6 6.3 %fusion.15 = f32[1024,64]{0,1:T(8,128)S(1)} fusion(f32[1024,1024]{1,0:T(8,128)} %all-reduce.5.cloned.1.call-done, f32[1024,64]{0,1:T(8,128)S(1)} %copy-done), kind=kOutput, calls=%fused_computation.21 | convolution fusion | flops 805306368 | bytes 4718592 | tf_op jit(solution)/shard_map/dot_general | solution.py:30
  593.4 5.8 cholesky.16
  600.6 4.9 custom-call.7
  605.9 2.5 fusion.5
  (28 shorter events, 4.3 us)
Async XLA Ops:
  7.2 579.4 %copy-start = (f32[1024,64]{0,1:T(8,128)S(1)}, f32[1024,64]{0,1:T(8,128)}, u32[]{:S(2)}) copy-start(f32[1024,64]{0,1:T(8,128)} %param.9) | copy-start | bytes 786436
  7.2 5.5 copy-start.4
  44.5 4.4 copy-start.5
  44.5 31.1 %all-to-all-start = ((f32[4,1,131072]{2,1,0:T(1,128)}), f32[4,1,131072]{2,1,0:T(1,128)S(1)}, u32[]{:S(2)}, u32[]{:S(2)}) async-start(f32[4,1,131072]{2,1,0:T(1,128)} %reshape.31), calls=%async_computation | async-start | bytes 4194304 | tf_op jit(solution)/shard_map/all_to_all | solution.py:17
  75.5 1.4 copy-start.2
  174.0 6.8 %copy-start.6 = (f32[4,32]{1,0:T(4,128)S(1)}, f32[4,32]{1,0:T(4,128)}, u32[]{:S(2)}) copy-start(f32[4,32]{1,0:T(4,128)} %param.7) | copy-start | bytes 1540
  174.0 73.3 %all-to-all-start.2 = ((f32[8,1,65536]{2,1,0:T(1,128)}), f32[8,1,65536]{2,1,0:T(1,128)}, u32[]{:S(2)}, u32[]{:S(2)}) async-start(f32[8,1,65536]{2,1,0:T(1,128)} %reshape.33), calls=%async_computation.2 | async-start | bytes 4194304 | tf_op jit(solution)/shard_map/all_to_all | solution.py:21
  180.8 245.5 %all-reduce.3.cloned.1.call-start = ((), (), s32[]{:S(2)}) async-start(), calls=%async_computation.4 | async-start | bytes 8388608 | tf_op jit(solution)/shard_map/psum | solution.py:29
  342.4 244.2 %all-reduce.5.cloned.1.call-start = ((), (), s32[]{:S(2)}) async-start(), calls=%async_computation.5 | async-start | bytes 8388608 | tf_op jit(solution)/shard_map/psum | solution.py:29
  428.2 177.7 %copy-start.1 = (f32[64,8,8,128]{3,1,2,0:T(8,128)S(1)}, f32[64,8,8,128]{3,1,2,0:T(8,128)}, u32[]{:S(2)}) copy-start(f32[64,8,8,128]{3,1,2,0:T(8,128)} %copy.41) | copy-start | bytes 6291460
  605.9 2.5 copy-start.3
Sparse Core Ops, SparseCore 0:
  342.6 83.7 all-reduce.2
  430.0 156.5 all-reduce.4
